TPU v7x, 512 devices: a 8x2x16 block of a 8x16x16 slice. The times are simulated.
512 devices in a mesh: groups: 2 (over y), seq: 32 (over z, core), rep: 8 (over x).
Axes of the slice: x: 8, y: 2, z: 16, core: 2. Of those that a mesh axis runs over, the one named last changes fastest.
The devices are a block of a 8x16x16 slice.
Arguments:
- queries: bfloat16 [1024, 4096], P(('groups', 'seq'), 'rep'), parts along dimension 0, may hold values from -128 to 128
- keys_new: bfloat16 [1024, 1024], P(('groups', 'seq'), 'rep'), parts along dimension 0, may hold values from -4 to 4
- values_new: bfloat16 [1024, 1024], P(('groups', 'seq'), 'rep'), parts along dimension 0, may hold values from -6 to 6
- keys_past: bfloat16 [16384, 1024], P(('groups', 'seq'), 'rep'), parts along dimension 0, may hold values from -4 to 4
- values_past: bfloat16 [16384, 1024], P(('groups', 'seq'), 'rep'), parts along dimension 0, may hold values from -6 to 6
- block_order: int32 [64], P('groups'), parts along dimension 0, may hold values from 0 to 31, each once
- residual: bfloat16 [1024, 4096], P(('groups', 'seq'), 'rep'), parts along dimension 0, may hold values from -6 to 6
- out_proj: bfloat16 [4096, 4096], P('seq', 'rep'), may hold values from -0.09375 to 0.09375
- norm_gain: float32 [4096], replicated, may hold values from 0.5 to 1.5
- router: float32 [4096, 4], replicated, may hold values from -0.09375 to 0.09375
- w_gate: bfloat16 [8, 4096, 4096], P('rep', None, 'seq'), may hold values from -0.09375 to 0.09375
- w_up: bfloat16 [8, 4096, 4096], P('rep', None, 'seq'), may hold values from -0.09375 to 0.09375
- w_down: bfloat16 [8, 4096, 4096], P('rep', 'seq'), may hold values from -0.0625 to 0.0625
- expert_ids: int32 [1024, 2], P(('groups', 'seq')), parts along dimension 0, may hold values from 0 to 3, all different within a row; in each aligned block of 16 rows (0 to 15, 16 to 31, ...) at most 12 rows name the same one
Outputs:
- attended: bfloat16 [1024, 4096], P(('groups', 'seq'), 'rep'), parts along dimension 0
- layer_out: bfloat16 [1024, 4096], P(('groups', 'seq'), 'rep'), parts along dimension 0
- keys_cache: bfloat16 [1024, 1024], P(('groups', 'seq')), parts along dimension 0
- values_cache: bfloat16 [1024, 1024], P(('groups', 'seq')), parts along dimension 0
There are 2 independent parts, one for each index of `groups`. A program takes and returns all parts, laid end to end along the dimension named above; an argument that names none is the same for every part. Nothing has to cross between parts.
Inputs may be any that keep to these rules, and one draw needn't show every extreme that they name: `block_order`: each block index 0 to 32 - 1 appears once. `expert_ids`: each row names 2 different experts; in the rows of one device (aligned blocks of 16 rows) no expert is named by more than 12 rows, and in some block one expert is named by exactly 12.
All inputs are finite; a program needn't handle non-finite values.
Results may differ from a plain program's by a relative error of at most 0.011.
Values may be sent and summed in bfloat16 or wider, within the bound.
A program may use at most 64 MiB of HBM per device.

v0:
```python
import math
import jax
import jax.numpy as jnp
from jax import lax
from jax.sharding import Mesh
from jax.sharding import PartitionSpec as P

EXPERTS = 4
CAP = 12
SEQ = ("seq_0", "seq_1")
GROUPS_SEQ = ("groups", "seq_0", "seq_1")


def in_one_piece(arrays, axis, dim, along):
    both = jnp.concatenate(arrays, axis=along)
    out, at, gathered = (lax.all_gather(both, axis, axis=dim, tiled=True), 0, [])
    for a in arrays:
        gathered.append(lax.slice_in_dim(out, at, at + a.shape[along], axis=along))
        at += a.shape[along]
    return tuple(gathered)


def sent_to_all(array, axis):
    size = lax.axis_size(axis)
    return lax.all_to_all(
        jnp.broadcast_to(array[None], (size, *array.shape)), axis, 0, 0, tiled=True
    )


def laid_out(tiles, dim):
    tiles = jnp.moveaxis(tiles, 0, dim)
    shape = tiles.shape
    return tiles.reshape(*shape[:dim], shape[dim] * shape[dim + 1], *shape[dim + 2 :])


def gather_directly(array, axis, dim):
    tiles = sent_to_all(array, axis)
    return laid_out(tiles, dim)


def own_block(tiles, axes, order):
    shape = [lax.axis_size(a) for a in axes]
    tiles = tiles.reshape(*shape, *tiles.shape[1:])
    tiles = tiles.transpose(*order, *range(len(axes), tiles.ndim))
    tiles = tiles.reshape(-1, *tiles.shape[len(axes) :])
    for k in order:
        tiles = lax.psum_scatter(tiles, axes[k], scatter_dimension=0, tiled=True)
    return tiles[0]


def in_blocks(array, dim, size):
    shape = array.shape
    tiles = array.reshape(*shape[:dim], size, shape[dim] // size, *shape[dim + 1 :])
    return jnp.moveaxis(tiles, dim, 0)


def sum_by_axis(array, axes, order, dim):
    size = lax.axis_size(axes)
    return own_block(in_blocks(array, dim, size), axes, order)


def block_lookup(owners, block_order):
    width = block_order.shape[0]
    hits = owners[:, None] == jnp.arange(width, dtype=jnp.int32)[None, :]
    return jnp.sum(jnp.where(hits, block_order[None, :], 0), axis=1)


def body(
    queries,
    keys_new,
    values_new,
    keys_past,
    values_past,
    block_order,
    residual,
    out_proj,
    norm_gain,
    router,
    w_gate,
    w_up,
    w_down,
    expert_ids,
):
    seq_index = lax.axis_index(SEQ)
    rep_index = lax.axis_index("rep")
    rep_count = lax.axis_size("rep")
    tok_count = queries.shape[0]
    head_dim = keys_new.shape[1]
    q_per = queries.shape[1] // head_dim
    past_len = keys_past.shape[0]
    key_span = past_len + tok_count
    row_total = tok_count * q_per
    my_block = block_lookup(jnp.full((1,), seq_index, jnp.int32), block_order)[0]
    scaling = 1.0 / math.sqrt(head_dim)
    query_rows = queries.reshape(row_total, head_dim)
    query_pos = my_block * tok_count + jnp.arange(row_total, dtype=jnp.int32) // q_per
    keys_local = jnp.concatenate([keys_past, keys_new], axis=0)
    values_local = jnp.concatenate([values_past, values_new], axis=0)
    running = jnp.full((row_total,), -1e30, jnp.float32)
    key_piece, value_piece = in_one_piece((keys_local, values_local), SEQ, 0, 1)
    row_count = key_piece.shape[0]
    key_index = jnp.arange(row_count, dtype=jnp.int32)
    key_owner = key_index // key_span
    offset = key_index % key_span
    key_pos = block_lookup(key_owner, block_order) * tok_count + offset - past_len
    visible = (offset < past_len)[None, :] | (key_pos[None, :] <= query_pos[:, None])
    scores = jnp.dot(query_rows, key_piece.T, preferred_element_type=jnp.float32) * scaling
    highest = jnp.maximum(running, jnp.max(jnp.where(visible, scores, -1e30), axis=1))
    weights = jnp.where(visible, jnp.exp(scores - highest[:, None]), 0.0)
    totals = jnp.sum(weights, axis=1)
    numerator = jnp.dot(
        weights.astype(jnp.bfloat16), value_piece, preferred_element_type=jnp.float32
    )
    running, totals, numerator = (highest, totals, numerator)
    attn_local = (
        (numerator / totals[:, None]).reshape(tok_count, q_per * head_dim).astype(jnp.bfloat16)
    )
    attn_full, keys_cache, values_cache = (
        lax.all_gather(attn_local, "rep", axis=1, tiled=True),
        *in_one_piece((keys_new, values_new), "rep", 1, 0),
    )
    projected = jnp.dot(
        attn_full,
        lax.all_gather(out_proj, SEQ, axis=0, tiled=True),
        preferred_element_type=jnp.float32,
    )
    attended = (residual.astype(jnp.float32) + projected).astype(jnp.bfloat16)
    full_rows = gather_directly(attended, "rep", 1)
    features = full_rows.astype(jnp.float32)
    mean_square = jnp.mean(features * features, axis=1, keepdims=True)
    normed = (features * norm_gain[None, :] * lax.rsqrt(mean_square + 1e-05)).astype(jnp.bfloat16)
    logits = jnp.dot(normed.astype(jnp.float32), router, precision=lax.Precision.HIGHEST)
    expert_range = jnp.arange(EXPERTS, dtype=jnp.int32)
    first_pick = (expert_ids[:, 0:1] == expert_range[None, :]).astype(jnp.float32)
    second_pick = (expert_ids[:, 1:2] == expert_range[None, :]).astype(jnp.float32)
    share_first = jax.nn.sigmoid(
        jnp.sum(first_pick * logits, axis=1) - jnp.sum(second_pick * logits, axis=1)
    )
    token_share = share_first[:, None] * first_pick + (1.0 - share_first)[:, None] * second_pick
    member = first_pick + second_pick
    ranking = jnp.cumsum(member, axis=0) - member
    slot_range = jnp.arange(CAP, dtype=jnp.float32)
    selection = member.T[:, None, :] * (ranking.T[:, None, :] == slot_range[None, :, None]).astype(
        jnp.float32
    )
    mine_mask = (expert_range == rep_index % EXPERTS).astype(jnp.float32)
    my_selection = jnp.einsum("e,ejt->jt", mine_mask, selection)
    slot_rows = jnp.dot(
        my_selection.astype(jnp.bfloat16), normed, preferred_element_type=jnp.float32
    ).astype(jnp.bfloat16)
    gate_local = w_gate[0]
    up_local = w_up[0]
    down_local = w_down[0]
    piece = lax.all_gather(slot_rows, SEQ, axis=0, tiled=True)
    gate_part = jnp.dot(piece, gate_local, preferred_element_type=jnp.float32)
    up_part = jnp.dot(piece, up_local, preferred_element_type=jnp.float32)
    hidden_slots = (jax.nn.silu(gate_part) * up_part).astype(jnp.bfloat16)
    expert_part = sum_by_axis(
        jnp.dot(hidden_slots, down_local, preferred_element_type=jnp.float32).astype(jnp.bfloat16),
        SEQ,
        (1, 0),
        0,
    ).astype(jnp.float32)
    returned = lax.all_to_all(
        expert_part.astype(jnp.bfloat16), "rep", split_axis=1, concat_axis=0, tiled=True
    ).astype(expert_part.dtype)
    source_expert = jnp.arange(rep_count, dtype=jnp.int32) % EXPERTS
    source_pick = (source_expert[:, None] == expert_range[None, :]).astype(jnp.float32)
    combine = jnp.einsum("re,ejt,te->trj", source_pick, selection, token_share).reshape(
        tok_count, rep_count * CAP
    )
    moe_slice = jnp.dot(combine, returned, precision=lax.Precision.HIGHEST)
    layer_out = (attended.astype(jnp.float32) + moe_slice).astype(jnp.bfloat16)
    return (attended, layer_out, keys_cache, values_cache)


def solution(mesh):
    split = Mesh(
        mesh.devices.reshape(mesh.shape["groups"], 16, 2, mesh.shape["rep"]),
        ("groups", "seq_0", "seq_1", "rep"),
    )
    return jax.shard_map(
        body,
        mesh=split,
        in_specs=(
            P(GROUPS_SEQ, "rep"),
            P(GROUPS_SEQ, "rep"),
            P(GROUPS_SEQ, "rep"),
            P(GROUPS_SEQ, "rep"),
            P(GROUPS_SEQ, "rep"),
            P("groups"),
            P(GROUPS_SEQ, "rep"),
            P(SEQ, "rep"),
            P(),
            P(),
            P("rep", None, SEQ),
            P("rep", None, SEQ),
            P("rep", SEQ, None),
            P(GROUPS_SEQ, None),
        ),
        out_specs=(
            P(GROUPS_SEQ, "rep"),
            P(GROUPS_SEQ, "rep"),
            P(GROUPS_SEQ, None),
            P(GROUPS_SEQ, None),
        ),
        check_vma=False,
    )
```

profile of v0, /device:TPU:66, one launch (start us, length us, event | category | flops | bytes accessed | tf_op | source)
XLA Modules:
  0.0 435.2 jit_solution(9324647808169427397)
XLA Ops:
  7.2 0.0 copy-start
  7.2 0.1 all-gather.5.cloned.1.call-start
  7.3 1.7 maximum_maximum_fusion
  8.9 0.1 all-gather.5.cloned.1.call-update
  9.0 0.1 all-gather.7.cloned.1.call-start
  9.0 0.7 all-gather.7.cloned.1.call-update
  9.8 0.7 reshape.156
  10.5 1.3 fusion.64
  12.5 0.9 select_reduce_fusion.1
  13.5 106.4 %all-gather.5.cloned.1.call-done = bf16[8704,256]{1,0:T(8,128)(2,1)} async-done(((bf16[272,256]{1,0:T(8,128)(2,1)}), bf16[8704,256]{1,0:T(8,128)(2,1)}) %all-gather.5.cloned.1.call-update) | async-done | bytes 4456464 | tf_op jit(solution)/shard_map/all_gather | solution.py:16
  119.9 2.8 select_reduce_fusion
  122.7 0.9 fusion.5
  123.6 0.0 copy-start.6
  123.6 0.8 fusion.22
  124.5 24.7 %all_gather.16 = bf16[16,4096]{1,0:T(8,128)(2,1)S(1)} all-gather(bf16[16,512]{1,0:T(8,128)(2,1)S(1)} %convert_element_type.81), channel_id=1, replica_groups=mesh['groups'=2,'seq_0'=16,'seq_1'=2,'rep'=8] {'rep'}, dimensions={1}, use_global_device_ids=true | all-gather | bytes 147456 | tf_op jit(solution)/shard_map/all_gather | solution.py:119
  149.2 44.8 %all-gather.7.cloned.1.call-done = bf16[4096,512]{1,0:T(8,128)(2,1)} async-done(((bf16[128,512]{1,0:T(8,128)(2,1)}), bf16[4096,512]{1,0:T(8,128)(2,1)}) %all-gather.7.cloned.1.call-update) | async-done | bytes 4194320 | tf_op jit(solution)/shard_map/all_gather | solution.py:124
  194.0 2.8 fusion.16
  196.8 0.7 broadcast_in_dim.33
  197.5 7.2 %all-to-all-start = ((bf16[8,16,512]{2,1,0:T(8,128)(2,1)}), bf16[8,16,512]{2,1,0:T(8,128)(2,1)S(1)}, u32[]{:S(2)}, u32[]{:S(2)}) async-start(bf16[8,16,512]{2,1,0:T(8,128)(2,1)} %broadcast_in_dim.33), calls=%async_computation | async-start | bytes 262144 | tf_op jit(solution)/shard_map/all_to_all | solution.py:25
  204.8 8.0 %all-to-all-done = bf16[8,16,512]{2,1,0:T(8,128)(2,1)S(1)} async-done(((bf16[8,16,512]{2,1,0:T(8,128)(2,1)}), bf16[8,16,512]{2,1,0:T(8,128)(2,1)S(1)}, u32[]{:S(2)}, u32[]{:S(2)}) %all-to-all-start) | async-done | bytes 131104 | tf_op jit(solution)/shard_map/all_to_all | solution.py:25
  212.8 0.1 fusion.32
  213.0 0.3 select_reduce_fusion.2
  213.3 0.1 copy.48
  213.5 0.1 copy.49
  213.5 0.1 fusion.47
  213.7 0.9 fusion.1
  214.6 0.1 all-gather.9.cloned.1.call-update
  214.6 0.1 reduce-scatter.3.cloned.1.call-start
  214.7 68.2 %all-gather.9.cloned.1.call-done = bf16[32,12,4096]{2,1,0:T(8,128)(2,1)} async-done(((bf16[1,12,4096]{2,1,0:T(8,128)(2,1)}), bf16[32,12,4096]{2,1,0:T(8,128)(2,1)}) %all-gather.9.cloned.1.call-update) | async-done | bytes 3145744 | tf_op jit(solution)/shard_map/all_gather | solution.py:154
  282.9 5.6 %reshape.160 = bf16[384,4096]{1,0:T(8,128)(2,1)} reshape(bf16[32,12,4096]{2,1,0:T(8,128)(2,1)} %all-gather.9.cloned.1.call-done) | data formatting | bytes 6291456
  288.5 2.9 fusion.30
  291.5 7.0 %convolution_convert_fusion = bf16[384,4096]{1,0:T(8,128)(2,1)} fusion(bf16[384,4096]{1,0:T(8,128)(2,1)} %reshape.160, bf16[1,128,4096]{2,1,0:T(8,128)(2,1)S(1)} %copy-done, bf16[1,4096,128]{2,1,0:T(8,128)(2,1)S(1)} %copy-done.2, f32[384,128]{1,0:T(8,128)S(1)} %fusion.30), kind=kOutput, calls=%fused_computation.2 | convolution fusion | flops 807174144 | bytes 8585216 | tf_op jit(solution)/shard_map/dot_general | solution.py:159
  298.5 5.5 %reshape_reshape.3 = bf16[16,2,12,4096]{3,2,1,0:T(8,128)(2,1)} reshape(bf16[384,4096]{1,0:T(8,128)(2,1)} %convolution_convert_fusion) | data formatting | bytes 6291456 | tf_op jit(solution)/shard_map/reshape;reshape | solution.py:43
  304.0 5.6 %copy.51 = bf16[2,16,12,4096]{3,1,0,2:T(8,128)(2,1)} copy(bf16[2,16,12,4096]{3,2,0,1:T(8,128)(2,1)} %bitcast.62) | data formatting | bytes 6291456 | tf_op jit(solution)/shard_map/transpose | solution.py:44
  309.6 0.1 reduce-scatter.3.cloned.1.call-update
  309.7 0.2 reduce-scatter.5.cloned.1.call-start
  309.9 19.5 %reduce-scatter.3.cloned.1.call-done = bf16[16,12,4096]{2,0,1:T(8,128)(2,1)} async-done(((bf16[32,12,4096]{2,0,1:T(8,128)(2,1)}), bf16[16,12,4096]{2,0,1:T(8,128)(2,1)}) %reduce-scatter.3.cloned.1.call-update) | async-done | bytes 1572880 | tf_op jit(solution)/shard_map/reduce_scatter | solution.py:47
  329.5 3.7 copy.52
  333.1 0.1 reduce-scatter.5.cloned.1.call-update
  333.2 22.3 %all_gather.19 = bf16[32,1024]{1,0:T(8,128)(2,1)S(1)} all-gather(bf16[32,128]{1,0:T(8,128)(2,1)S(1)} %pad_maximum_fusion), channel_id=1, replica_groups=mesh['groups'=2,'seq_0'=16,'seq_1'=2,'rep'=8] {'rep'}, dimensions={1}, use_global_device_ids=true | all-gather | bytes 73728 | tf_op jit(solution)/shard_map/all_gather | solution.py:16
  355.6 0.6 fusion.72
  356.2 54.9 %reduce-scatter.5.cloned.1.call-done = bf16[1,12,4096]{2,1,0:T(8,128)(2,1)} async-done(((bf16[16,12,4096]{2,1,0:T(8,128)(2,1)}), bf16[1,12,4096]{2,1,0:T(8,128)(2,1)}) %reduce-scatter.5.cloned.1.call-update) | async-done | bytes 98320 | tf_op jit(solution)/shard_map/reduce_scatter | solution.py:47
  411.1 0.9 copy.57
  412.0 0.7 copy.53
  412.7 7.4 %all-to-all-start.1 = ((bf16[12,8,512]{2,0,1:T(8,128)(2,1)}), bf16[12,8,512]{2,0,1:T(8,128)(2,1)S(1)}, u32[]{:S(2)}, u32[]{:S(2)}) async-start(bf16[12,8,512]{2,0,1:T(8,128)(2,1)} %copy.53), calls=%async_computation.3 | async-start | bytes 262144 | tf_op jit(solution)/shard_map/all_to_all | solution.py:164
  420.2 0.2 convolution_bitcast_fusion
  420.4 7.4 %all-to-all-done.1 = bf16[12,8,512]{2,0,1:T(8,128)(2,1)S(1)} async-done(((bf16[12,8,512]{2,0,1:T(8,128)(2,1)}), bf16[12,8,512]{2,0,1:T(8,128)(2,1)S(1)}, u32[]{:S(2)}, u32[]{:S(2)}) %all-to-all-start.1) | async-done | bytes 98336 | tf_op jit(solution)/shard_map/all_to_all | solution.py:164
  427.8 0.8 fusion.15
  (38 shorter events, 0.3 us)
Async XLA Ops:
  7.2 284.3 %copy-start = (bf16[1,128,4096]{2,1,0:T(8,128)(2,1)S(1)}, bf16[1,128,4096]{2,1,0:T(8,128)(2,1)}, u32[]{:S(2)}) copy-start(bf16[1,128,4096]{2,1,0:T(8,128)(2,1)} %param.26) | copy-start | bytes 3145732
  7.2 112.7 %all-gather.5.cloned.1.call-start = ((), (), s32[]{:S(2)}) async-start(), calls=%async_computation.4 | async-start | bytes 4595712 | tf_op jit(solution)/shard_map/all_gather | solution.py:16
  9.0 185.0 %all-gather.7.cloned.1.call-start = ((), (), s32[]{:S(2)}) async-start(), calls=%async_computation.5 | async-start | bytes 4325376 | tf_op jit(solution)/shard_map/all_gather | solution.py:124
  119.9 3.7 copy-start.10
  123.6 70.4 %copy-start.6 = (bf16[16,512]{1,0:T(8,128)(2,1)S(1)}, bf16[16,512]{1,0:T(8,128)(2,1)}, u32[]{:S(2)}) copy-start(bf16[16,512]{1,0:T(8,128)(2,1)} %param.20) | copy-start | bytes 49156
  149.2 55.5 %copy-start.9 = (s32[16,2]{0,1:T(2,128)S(1)}, s32[16,2]{0,1:T(2,128)}, u32[]{:S(2)}) copy-start(s32[16,2]{0,1:T(2,128)} %param.27) | copy-start | bytes 388
  149.2 63.7 %copy-start.4 = (f32[4096,4]{0,1:T(4,128)S(1)}, f32[4096,4]{0,1:T(4,128)}, u32[]{:S(2)}) copy-start(f32[4096,4]{0,1:T(4,128)} %param.23) | copy-start | bytes 196612
  149.2 63.8 %copy-start.5 = (f32[4096]{0:T(1024)S(1)}, f32[4096]{0:T(1024)}, u32[]{:S(2)}) copy-start(f32[4096]{0:T(1024)} %param.22) | copy-start | bytes 49156
  196.8 231.0 %copy-start.3 = (bf16[16,512]{1,0:T(8,128)(2,1)}, bf16[16,512]{1,0:T(8,128)(2,1)S(1)}, u32[]{:S(2)}) copy-start(bf16[16,512]{1,0:T(8,128)(2,1)S(1)} %fusion.16) | copy-start | bytes 49156
  197.5 15.2 %all-to-all-start = ((bf16[8,16,512]{2,1,0:T(8,128)(2,1)}), bf16[8,16,512]{2,1,0:T(8,128)(2,1)S(1)}, u32[]{:S(2)}, u32[]{:S(2)}) async-start(bf16[8,16,512]{2,1,0:T(8,128)(2,1)} %broadcast_in_dim.33), calls=%async_computation | async-start | bytes 262144 | tf_op jit(solution)/shard_map/all_to_all | solution.py:25
  204.7 78.2 %all-gather.9.cloned.1.call-start = ((), (), s32[]{:S(2)}) async-start(), calls=%async_computation.8 | async-start | bytes 4325376 | tf_op jit(solution)/shard_map/all_gather | solution.py:154
  214.6 73.9 %copy-start.1 = (bf16[1,4096,128]{2,1,0:T(8,128)(2,1)S(1)}, bf16[1,4096,128]{2,1,0:T(8,128)(2,1)}, u32[]{:S(2)}) copy-start(bf16[1,4096,128]{2,1,0:T(8,128)(2,1)} %param.24) | copy-start | bytes 3145732
  214.6 114.8 %reduce-scatter.3.cloned.1.call-start = ((), (), s32[]{:S(2)}) async-start(), calls=%async_computation.6 | async-start | bytes 4718592 | tf_op jit(solution)/shard_map/reduce_scatter | solution.py:47
  288.5 3.0 copy-start.2
  309.7 23.5 %copy-start.7 = (bf16[16,128]{1,0:T(8,128)(2,1)S(1)}, bf16[16,128]{1,0:T(8,128)(2,1)}, u32[]{:S(2)}) copy-start(bf16[16,128]{1,0:T(8,128)(2,1)} %param.16) | copy-start | bytes 12292
  309.7 23.5 %copy-start.8 = (bf16[16,128]{1,0:T(8,128)(2,1)S(1)}, bf16[16,128]{1,0:T(8,128)(2,1)}, u32[]{:S(2)}) copy-start(bf16[16,128]{1,0:T(8,128)(2,1)} %param.15) | copy-start | bytes 12292
  309.7 101.4 %reduce-scatter.5.cloned.1.call-start = ((), (), s32[]{:S(2)}) async-start(), calls=%async_computation.7 | async-start | bytes 2228224 | tf_op jit(solution)/shard_map/reduce_scatter | solution.py:47
  412.7 15.1 %all-to-all-start.1 = ((bf16[12,8,512]{2,0,1:T(8,128)(2,1)}), bf16[12,8,512]{2,0,1:T(8,128)(2,1)S(1)}, u32[]{:S(2)}, u32[]{:S(2)}) async-start(bf16[12,8,512]{2,0,1:T(8,128)(2,1)} %copy.53), calls=%async_computation.3 | async-start | bytes 262144 | tf_op jit(solution)/shard_map/all_to_all | solution.py:164
Sparse Core Ops, SparseCore 0:
  10.2 109.7 all-gather.4
  122.1 71.8 all-gather.6
  214.7 68.1 all-gather.8
  309.8 19.6 reduce-scatter.2
  333.3 77.7 reduce-scatter.4
where the time goes:
time: 436 us; the launch traced here: 435 us
  waiting for transfers between devices  310 us (71%)
  blocking collectives  47 us (11%)
  local copies, waits for them, and re-layouts  24.3 us (6%)
  matrix products  18.8 us (4%)
  starting transfers between devices  15.1 us (3%)
  between operations  14.7 us (3%)
  other arithmetic  5.04 us (1%)
    all_gather x1, waiting for transfers between devices, in_one_piece(): lax.all_gather(both, axis, axis=dim, tiled=True)  106 us
    reduce_scatter x2, waiting for transfers between devices, own_block(): tiles = lax.psum_scatter(tiles, axes[k], scatter_dimension=0, tiled=True)  74.4 us
    all_gather x1, waiting for transfers between devices, body(): piece = lax.all_gather(slot_rows, SEQ, axis=0, tiled=True)  68.2 us
    all_gather x1, waiting for transfers between devices, body(): lax.all_gather(out_proj, SEQ, axis=0, tiled=True)  44.8 us
    all_gather x1, blocking collectives, body(): lax.all_gather(attn_local, 'rep', axis=1, tiled=True)  24.7 us
    all_gather x1, blocking collectives, in_one_piece(): lax.all_gather(both, axis, axis=dim, tiled=True)  22.3 us
  transfers between devices with their start and end apart: 7, of which 7 were waited for; matrix products, arithmetic and copies ran while one was open for 2% of the time, Pallas kernels for 0%

commit v1 on v0

--- a/solution.py
+++ b/solution.py
@@ -9,6 +9,13 @@
 CAP = 12
 SEQ = ("seq_0", "seq_1")
 GROUPS_SEQ = ("groups", "seq_0", "seq_1")
+
+
+def exchange_gather(array, axis, d):
+    devices = lax.axis_size(axis)
+    blocks = jnp.stack([array for _ in range(devices)])
+    blocks = lax.all_to_all(blocks, axis, split_axis=0, concat_axis=0)
+    return jnp.concatenate(blocks, axis=d)
 
 
 def in_one_piece(arrays, axis, dim, along):
@@ -120,9 +127,7 @@
         *in_one_piece((keys_new, values_new), "rep", 1, 0),
     )
     projected = jnp.dot(
-        attn_full,
-        lax.all_gather(out_proj, SEQ, axis=0, tiled=True),
-        preferred_element_type=jnp.float32,
+        attn_full, exchange_gather(out_proj, SEQ, 0), preferred_element_type=jnp.float32
     )
     attended = (residual.astype(jnp.float32) + projected).astype(jnp.bfloat16)
     full_rows = gather_directly(attended, "rep", 1)

time: 436 us -> 506 us (1.16)
  starting transfers between devices: 15.1 us -> 64.5 us
  waiting for transfers between devices: 310 us -> 331 us
    all_gather x1, waiting for transfers between devices: 106 us -> 158 us  [in_one_piece(): lax.all_gather(both, axis, axis=dim, tiled=True)]
    all_gather x1 -> x0, waiting for transfers between devices: 44.8 us -> none  [body(): lax.all_gather(out_proj, SEQ, axis=0, tiled=True)]
    all_to_all x0 -> x1, starting transfers between devices: none -> 44.6 us  [exchange_gather(): blocks = lax.all_to_all(blocks, axis, split_axis=0, concat_axis=0)]
    all_to_all x0 -> x1, waiting for transfers between devices: none -> 16.6 us  [exchange_gather(): blocks = lax.all_to_all(blocks, axis, split_axis=0, concat_axis=0)]
  transfers between devices with their start and end apart: 7 -> 7, of which waited for: 7 -> 7; matrix products, arithmetic and copies ran while one was open for 2% -> 1% of each run, Pallas kernels for 0% -> 0%
where the time goes in v1:
time: 506 us; the launch traced here: 505 us
  waiting for transfers between devices  331 us (65%)
  starting transfers between devices  64.5 us (13%)
  blocking collectives  46.3 us (9%)
  local copies, waits for them, and re-layouts  27 us (5%)
  matrix products  18.8 us (4%)
  between operations  14.7 us (3%)
    all_gather x1, waiting for transfers between devices, in_one_piece(): lax.all_gather(both, axis, axis=dim, tiled=True)  158 us
    reduce_scatter x2, waiting for transfers between devices, own_block(): tiles = lax.psum_scatter(tiles, axes[k], scatter_dimension=0, tiled=True)  74.6 us
    all_gather x1, waiting for transfers between devices, body(): piece = lax.all_gather(slot_rows, SEQ, axis=0, tiled=True)  66.1 us
    all_to_all x1, starting transfers between devices, exchange_gather(): blocks = lax.all_to_all(blocks, axis, split_axis=0, concat_axis=0)  44.6 us
    all_gather x1, blocking collectives, body(): lax.all_gather(attn_local, 'rep', axis=1, tiled=True)  24 us
    all_gather x1, blocking collectives, in_one_piece(): lax.all_gather(both, axis, axis=dim, tiled=True)  22.3 us
    all_to_all x1, waiting for transfers between devices, exchange_gather(): blocks = lax.all_to_all(blocks, axis, split_axis=0, concat_axis=0)  16.6 us
    all_to_all x1, starting transfers between devices, sent_to_all(): lax.all_to_all(jnp.broadcast_to(array[None], (size, *array.shape)), axis,...  12.1 us
  transfers between devices with their start and end apart: 7, of which 7 were waited for; matrix products, arithmetic and copies ran while one was open for 1% of the time, Pallas kernels for 0%

profile of v1, /device:TPU:66, one launch (start us, length us, event | category | flops | bytes accessed | tf_op | source)
XLA Modules:
  0.0 504.9 jit_solution(5374908904002814061)
XLA Ops:
  7.2 0.0 copy-start
  7.2 3.4 stack.2
  10.6 0.0 copy-start.11
  10.7 0.0 copy-start.13
  10.7 44.6 %all-to-all-start = ((bf16[32,128,512]{2,1,0:T(8,128)(2,1)}), bf16[32,128,512]{2,1,0:T(8,128)(2,1)}, u32[]{:S(2)}, u32[]{:S(2)}) async-start(bf16[32,128,512]{2,1,0:T(8,128)(2,1)} %stack.2), calls=%async_computation | async-start | bytes 8388608 | tf_op jit(solution)/shard_map/all_to_all | solution.py:17
  55.3 0.1 all-gather.4.cloned.1.call-start
  55.4 0.7 maximum_maximum_fusion
  56.1 0.1 all-gather.4.cloned.1.call-update
  56.2 0.6 fusion.64
  57.5 0.3 select_reduce_fusion.1
  57.8 158.2 %all-gather.4.cloned.1.call-done = bf16[8704,256]{1,0:T(8,128)(2,1)} async-done(((bf16[272,256]{1,0:T(8,128)(2,1)}), bf16[8704,256]{1,0:T(8,128)(2,1)}) %all-gather.4.cloned.1.call-update) | async-done | bytes 4456464 | tf_op jit(solution)/shard_map/all_gather | solution.py:23
  216.0 2.8 select_reduce_fusion
  218.8 0.9 fusion.5
  219.7 0.8 fusion.22
  220.6 24.0 %all_gather.13 = bf16[16,4096]{1,0:T(8,128)(2,1)S(1)} all-gather(bf16[16,512]{1,0:T(8,128)(2,1)S(1)} %convert_element_type.81), channel_id=1, replica_groups=mesh['groups'=2,'seq_0'=16,'seq_1'=2,'rep'=8] {'rep'}, dimensions={1}, use_global_device_ids=true | all-gather | bytes 147456 | tf_op jit(solution)/shard_map/all_gather | solution.py:126
  244.6 16.6 %all-to-all-done = bf16[32,128,512]{2,1,0:T(8,128)(2,1)} async-done(((bf16[32,128,512]{2,1,0:T(8,128)(2,1)}), bf16[32,128,512]{2,1,0:T(8,128)(2,1)}, u32[]{:S(2)}, u32[]{:S(2)}) %all-to-all-start) | async-done | bytes 4194336 | tf_op jit(solution)/shard_map/all_to_all | solution.py:17
  261.2 2.9 fusion.16
  264.0 0.7 broadcast_in_dim.33
  264.7 12.1 %all-to-all-start.1 = ((bf16[8,16,512]{2,1,0:T(8,128)(2,1)}), bf16[8,16,512]{2,1,0:T(8,128)(2,1)S(1)}, u32[]{:S(2)}, u32[]{:S(2)}) async-start(bf16[8,16,512]{2,1,0:T(8,128)(2,1)} %broadcast_in_dim.33), calls=%async_computation.1 | async-start | bytes 262144 | tf_op jit(solution)/shard_map/all_to_all | solution.py:32
  276.8 7.7 %all-to-all-done.1 = bf16[8,16,512]{2,1,0:T(8,128)(2,1)S(1)} async-done(((bf16[8,16,512]{2,1,0:T(8,128)(2,1)}), bf16[8,16,512]{2,1,0:T(8,128)(2,1)S(1)}, u32[]{:S(2)}, u32[]{:S(2)}) %all-to-all-start.1) | async-done | bytes 131104 | tf_op jit(solution)/shard_map/all_to_all | solution.py:32
  284.5 0.1 fusion.32
  284.7 0.3 select_reduce_fusion.2
  285.0 0.1 copy.48
  285.2 0.1 copy.49
  285.3 0.1 fusion.47
  285.4 0.9 fusion.1
  286.3 0.1 all-gather.6.cloned.1.call-update
  286.3 0.2 reduce-scatter.3.cloned.1.call-start
  286.6 66.1 %all-gather.6.cloned.1.call-done = bf16[32,12,4096]{2,1,0:T(8,128)(2,1)} async-done(((bf16[1,12,4096]{2,1,0:T(8,128)(2,1)}), bf16[32,12,4096]{2,1,0:T(8,128)(2,1)}) %all-gather.6.cloned.1.call-update) | async-done | bytes 3145744 | tf_op jit(solution)/shard_map/all_gather | solution.py:159
  352.7 5.6 %reshape.166 = bf16[384,4096]{1,0:T(8,128)(2,1)} reshape(bf16[32,12,4096]{2,1,0:T(8,128)(2,1)} %all-gather.6.cloned.1.call-done) | data formatting | bytes 6291456
  358.3 3.0 fusion.30
  361.3 7.0 %convolution_convert_fusion = bf16[384,4096]{1,0:T(8,128)(2,1)} fusion(bf16[384,4096]{1,0:T(8,128)(2,1)} %reshape.166, bf16[1,128,4096]{2,1,0:T(8,128)(2,1)S(1)} %copy-done, bf16[1,4096,128]{2,1,0:T(8,128)(2,1)S(1)} %copy-done.2, f32[384,128]{1,0:T(8,128)S(1)} %fusion.30), kind=kOutput, calls=%fused_computation.2 | convolution fusion | flops 807174144 | bytes 8585216 | tf_op jit(solution)/shard_map/dot_general | solution.py:164
  368.3 5.5 %reshape_reshape.3 = bf16[16,2,12,4096]{3,2,1,0:T(8,128)(2,1)} reshape(bf16[384,4096]{1,0:T(8,128)(2,1)} %convolution_convert_fusion) | data formatting | bytes 6291456 | tf_op jit(solution)/shard_map/reshape;reshape | solution.py:50
  373.8 5.6 %copy.51 = bf16[2,16,12,4096]{3,1,0,2:T(8,128)(2,1)} copy(bf16[2,16,12,4096]{3,2,0,1:T(8,128)(2,1)} %bitcast.63) | data formatting | bytes 6291456 | tf_op jit(solution)/shard_map/transpose | solution.py:51
  379.4 0.1 reduce-scatter.3.cloned.1.call-update
  379.4 0.1 reduce-scatter.5.cloned.1.call-start
  379.5 19.7 %reduce-scatter.3.cloned.1.call-done = bf16[16,12,4096]{2,0,1:T(8,128)(2,1)} async-done(((bf16[32,12,4096]{2,0,1:T(8,128)(2,1)}), bf16[16,12,4096]{2,0,1:T(8,128)(2,1)}) %reduce-scatter.3.cloned.1.call-update) | async-done | bytes 1572880 | tf_op jit(solution)/shard_map/reduce_scatter | solution.py:54
  399.3 3.6 copy.52
  402.9 0.1 reduce-scatter.5.cloned.1.call-update
  403.0 22.3 %all_gather.15 = bf16[32,1024]{1,0:T(8,128)(2,1)S(1)} all-gather(bf16[32,128]{1,0:T(8,128)(2,1)S(1)} %pad_maximum_fusion), channel_id=1, replica_groups=mesh['groups'=2,'seq_0'=16,'seq_1'=2,'rep'=8] {'rep'}, dimensions={1}, use_global_device_ids=true | all-gather | bytes 73728 | tf_op jit(solution)/shard_map/all_gather | solution.py:23
  425.3 0.6 fusion.72
  426.0 54.8 %reduce-scatter.5.cloned.1.call-done = bf16[1,12,4096]{2,1,0:T(8,128)(2,1)} async-done(((bf16[16,12,4096]{2,1,0:T(8,128)(2,1)}), bf16[1,12,4096]{2,1,0:T(8,128)(2,1)}) %reduce-scatter.5.cloned.1.call-update) | async-done | bytes 98320 | tf_op jit(solution)/shard_map/reduce_scatter | solution.py:54
  480.8 0.9 copy.57
  481.8 0.7 copy.53
  482.4 7.5 %all-to-all-start.2 = ((bf16[12,8,512]{2,0,1:T(8,128)(2,1)}), bf16[12,8,512]{2,0,1:T(8,128)(2,1)S(1)}, u32[]{:S(2)}, u32[]{:S(2)}) async-start(bf16[12,8,512]{2,0,1:T(8,128)(2,1)} %copy.53), calls=%async_computation.4 | async-start | bytes 262144 | tf_op jit(solution)/shard_map/all_to_all | solution.py:169
  489.9 0.2 convolution_bitcast_fusion
  490.1 7.4 %all-to-all-done.2 = bf16[12,8,512]{2,0,1:T(8,128)(2,1)S(1)} async-done(((bf16[12,8,512]{2,0,1:T(8,128)(2,1)}), bf16[12,8,512]{2,0,1:T(8,128)(2,1)S(1)}, u32[]{:S(2)}, u32[]{:S(2)}) %all-to-all-start.2) | async-done | bytes 98336 | tf_op jit(solution)/shard_map/all_to_all | solution.py:169
  497.6 0.8 fusion.15
  (46 shorter events, 0.3 us)
Async XLA Ops:
  7.2 354.1 %copy-start = (bf16[1,128,4096]{2,1,0:T(8,128)(2,1)S(1)}, bf16[1,128,4096]{2,1,0:T(8,128)(2,1)}, u32[]{:S(2)}) copy-start(bf16[1,128,4096]{2,1,0:T(8,128)(2,1)} %param.26) | copy-start | bytes 3145732
  10.6 44.7 %copy-start.4 = (bf16[256,128]{1,0:T(8,128)(2,1)S(1)}, bf16[256,128]{1,0:T(8,128)(2,1)}, u32[]{:S(2)}) copy-start(bf16[256,128]{1,0:T(8,128)(2,1)} %param.18) | copy-start | bytes 196612
  10.6 44.7 %copy-start.5 = (bf16[256,128]{1,0:T(8,128)(2,1)S(1)}, bf16[256,128]{1,0:T(8,128)(2,1)}, u32[]{:S(2)}) copy-start(bf16[256,128]{1,0:T(8,128)(2,1)} %param.17) | copy-start | bytes 196612
  10.6 44.7 %copy-start.9 = (bf16[16,128]{1,0:T(8,128)(2,1)S(1)}, bf16[16,128]{1,0:T(8,128)(2,1)}, u32[]{:S(2)}) copy-start(bf16[16,128]{1,0:T(8,128)(2,1)} %param.16) | copy-start | bytes 12292
  10.6 44.7 %copy-start.10 = (bf16[16,128]{1,0:T(8,128)(2,1)S(1)}, bf16[16,128]{1,0:T(8,128)(2,1)}, u32[]{:S(2)}) copy-start(bf16[16,128]{1,0:T(8,128)(2,1)} %param.15) | copy-start | bytes 12292
  10.6 45.5 %copy-start.11 = (bf16[16,512]{1,0:T(8,128)(2,1)S(1)}, bf16[16,512]{1,0:T(8,128)(2,1)}, u32[]{:S(2)}) copy-start(bf16[16,512]{1,0:T(8,128)(2,1)} %param.14) | copy-start | bytes 49156
  10.7 45.5 %copy-start.13 = (s32[32]{0:T(128)S(1)}, s32[32]{0:T(128)}, u32[]{:S(2)}) copy-start(s32[32]{0:T(128)} %param.19) | copy-start | bytes 388
  10.7 250.5 %all-to-all-start = ((bf16[32,128,512]{2,1,0:T(8,128)(2,1)}), bf16[32,128,512]{2,1,0:T(8,128)(2,1)}, u32[]{:S(2)}, u32[]{:S(2)}) async-start(bf16[32,128,512]{2,1,0:T(8,128)(2,1)} %stack.2), calls=%async_computation | async-start | bytes 8388608 | tf_op jit(solution)/shard_map/all_to_all | solution.py:17
  55.3 160.7 %all-gather.4.cloned.1.call-start = ((), (), s32[]{:S(2)}) async-start(), calls=%async_computation.5 | async-start | bytes 4595712 | tf_op jit(solution)/shard_map/all_gather | solution.py:23
  216.0 3.7 copy-start.14
  219.7 41.4 %copy-start.8 = (bf16[16,512]{1,0:T(8,128)(2,1)S(1)}, bf16[16,512]{1,0:T(8,128)(2,1)}, u32[]{:S(2)}) copy-start(bf16[16,512]{1,0:T(8,128)(2,1)} %param.20) | copy-start | bytes 49156
  261.1 15.6 %copy-start.12 = (s32[16,2]{0,1:T(2,128)S(1)}, s32[16,2]{0,1:T(2,128)}, u32[]{:S(2)}) copy-start(s32[16,2]{0,1:T(2,128)} %param.27) | copy-start | bytes 388
  261.2 23.5 %copy-start.6 = (f32[4096,4]{0,1:T(4,128)S(1)}, f32[4096,4]{0,1:T(4,128)}, u32[]{:S(2)}) copy-start(f32[4096,4]{0,1:T(4,128)} %param.23) | copy-start | bytes 196612
  261.2 23.5 %copy-start.7 = (f32[4096]{0:T(1024)S(1)}, f32[4096]{0:T(1024)}, u32[]{:S(2)}) copy-start(f32[4096]{0:T(1024)} %param.22) | copy-start | bytes 49156
  264.0 233.5 %copy-start.3 = (bf16[16,512]{1,0:T(8,128)(2,1)}, bf16[16,512]{1,0:T(8,128)(2,1)S(1)}, u32[]{:S(2)}) copy-start(bf16[16,512]{1,0:T(8,128)(2,1)S(1)} %fusion.16) | copy-start | bytes 49156
  264.7 19.8 %all-to-all-start.1 = ((bf16[8,16,512]{2,1,0:T(8,128)(2,1)}), bf16[8,16,512]{2,1,0:T(8,128)(2,1)S(1)}, u32[]{:S(2)}, u32[]{:S(2)}) async-start(bf16[8,16,512]{2,1,0:T(8,128)(2,1)} %broadcast_in_dim.33), calls=%async_computation.1 | async-start | bytes 262144 | tf_op jit(solution)/shard_map/all_to_all | solution.py:32
  276.8 76.0 %all-gather.6.cloned.1.call-start = ((), (), s32[]{:S(2)}) async-start(), calls=%async_computation.8 | async-start | bytes 4325376 | tf_op jit(solution)/shard_map/all_gather | solution.py:159
  286.3 72.0 %copy-start.1 = (bf16[1,4096,128]{2,1,0:T(8,128)(2,1)S(1)}, bf16[1,4096,128]{2,1,0:T(8,128)(2,1)}, u32[]{:S(2)}) copy-start(bf16[1,4096,128]{2,1,0:T(8,128)(2,1)} %param.24) | copy-start | bytes 3145732
  286.3 112.9 %reduce-scatter.3.cloned.1.call-start = ((), (), s32[]{:S(2)}) async-start(), calls=%async_computation.6 | async-start | bytes 4718592 | tf_op jit(solution)/shard_map/reduce_scatter | solution.py:54
  358.3 3.0 copy-start.2
  379.4 101.4 %reduce-scatter.5.cloned.1.call-start = ((), (), s32[]{:S(2)}) async-start(), calls=%async_computation.7 | async-start | bytes 2228224 | tf_op jit(solution)/shard_map/reduce_scatter | solution.py:54
  482.4 15.1 %all-to-all-start.2 = ((bf16[12,8,512]{2,0,1:T(8,128)(2,1)}), bf16[12,8,512]{2,0,1:T(8,128)(2,1)S(1)}, u32[]{:S(2)}, u32[]{:S(2)}) async-start(bf16[12,8,512]{2,0,1:T(8,128)(2,1)} %copy.53), calls=%async_computation.4 | async-start | bytes 262144 | tf_op jit(solution)/shard_map/all_to_all | solution.py:169
Sparse Core Ops, SparseCore 0:
  58.3 157.7 all-gather.3
  286.5 66.2 all-gather.5
  379.6 19.6 reduce-scatter.2
  403.1 77.6 reduce-scatter.4
